TPU v7x, 32 devices: a whole 2x2x4 slice. The times are simulated.
32 devices in a mesh: fsdp: 8 (over z, x), rep: 4 (over y, core).
Axes of the slice: x: 2, y: 2, z: 4, core: 2. Of those that a mesh axis runs over, the one named last changes fastest.
Arguments:
- partials: bfloat16 [4, 56, 1024, 1024], P('rep', None, 'fsdp'), may hold values from -400 to 400
- sketch: bfloat16 [8, 4, 2, 1024, 256], P('fsdp', 'rep'), may hold values from -3 to 3
- owner_table: int32 [56, 1], replicated, may hold values from 0 to 7; in each aligned block of 14 rows (0 to 13, 14 to 27, ...) at most 2 rows name the same one
Outputs:
- update: bfloat16 [56, 1024, 1024], P('rep', 'fsdp')
- new_sketch: bfloat16 [8, 4, 2, 1024, 256], P('fsdp', 'rep')
Inputs may be any that keep to these rules, and one draw needn't show every extreme that they name: `owner_table`: in each aligned slice of 14 blocks no owner holds more than 2 blocks; some owner holds exactly 2 in some slice.
All inputs are finite; a program needn't handle non-finite values.
Results may differ from a plain program's by a relative error of at most 0.015.
Values may be sent and summed in bfloat16 or wider, within the bound.
No kernel may reach another device: no remote copies, remote signals or barrier semaphores. Data moves between devices by JAX's collectives and lax.ppermute only.
A program may use at most 128 MiB of HBM per device.

v0:
```python
import math
import jax
import jax.numpy as jnp
from jax import lax
from jax.sharding import PartitionSpec as P

NS_ITERS = 5
DECAY = 0.9
DAMPING = 64.0
FIRST_AXES = (((0,), (0,)), ((), ()))
LAST_AXES = (((1,), (1,)), ((), ()))


def inverse_root(matrix, epsilon):
    identity = jnp.eye(matrix.shape[0], dtype=jnp.float32)
    trace_sum = jnp.trace(matrix) + epsilon
    current = matrix / trace_sum
    inverse = identity
    for repeat in range(NS_ITERS):
        middle = 1.5 * identity - 0.5 * jnp.dot(inverse, current, precision=lax.Precision.HIGHEST)
        current = jnp.dot(current, middle, precision=lax.Precision.HIGHEST)
        inverse = jnp.dot(middle, inverse, precision=lax.Precision.HIGHEST)
    return inverse / jnp.sqrt(trace_sum)


def precondition(gradient, current_sketch):
    identity = jnp.eye(current_sketch.shape[1], dtype=jnp.float32)
    projected = lax.dot_general(
        gradient, current_sketch, FIRST_AXES, preferred_element_type=jnp.float32
    ).astype(jnp.bfloat16)
    gram_matrix = lax.dot_general(
        current_sketch, current_sketch, FIRST_AXES, preferred_element_type=jnp.float32
    ).astype(jnp.bfloat16)
    powered = DECAY * jnp.dot(
        current_sketch, gram_matrix, preferred_element_type=jnp.float32
    ) + jnp.dot(gradient, projected, preferred_element_type=jnp.float32)
    inner_gram = lax.dot_general(powered, powered, FIRST_AXES, precision=lax.Precision.HIGHEST)
    basis_full = jnp.dot(powered, inverse_root(inner_gram, 1e-06), precision=lax.Precision.HIGHEST)
    basis_low = basis_full.astype(jnp.bfloat16)
    coefficients = lax.dot_general(
        gradient, basis_low, FIRST_AXES, preferred_element_type=jnp.float32
    ).astype(jnp.bfloat16)
    alignment = lax.dot_general(
        current_sketch, basis_low, FIRST_AXES, preferred_element_type=jnp.float32
    )
    energy = DECAY * lax.dot_general(
        alignment, alignment, FIRST_AXES, precision=lax.Precision.HIGHEST
    ) + lax.dot_general(coefficients, coefficients, FIRST_AXES, preferred_element_type=jnp.float32)
    root_inverse = inverse_root(energy + DAMPING * identity, 0.0)
    inner_part = jnp.dot(energy, root_inverse, precision=lax.Precision.HIGHEST)
    new_block = jnp.dot(basis_full, inner_part, precision=lax.Precision.HIGHEST).astype(
        jnp.bfloat16
    )
    mix_matrix = math.sqrt(DAMPING) * root_inverse - identity
    side_terms = lax.dot_general(
        coefficients.astype(jnp.float32), mix_matrix, LAST_AXES, precision=lax.Precision.HIGHEST
    ).astype(jnp.bfloat16)
    update_block = (
        gradient.astype(jnp.float32)
        + lax.dot_general(basis_low, side_terms, LAST_AXES, preferred_element_type=jnp.float32)
    ).astype(jnp.bfloat16)
    return (update_block, new_block)


def squared_sum(values):
    wide = values.astype(jnp.float32)
    return jnp.sum(wide * wide)


def process_slot(slot_index, arrived, clip_factor, held_sketches, filled):
    block_width = arrived.shape[-1]
    gradient = (clip_factor * arrived.reshape(block_width, block_width).astype(jnp.float32)).astype(
        jnp.bfloat16
    )
    current_sketch = held_sketches[slot_index]
    active = slot_index < filled
    update_block, new_block = precondition(gradient, current_sketch)
    new_block = jnp.where(active, new_block, current_sketch)
    return (update_block, new_block)


def local(partials, sketch, owner_table):
    block_total = partials.shape[1]
    row_count = partials.shape[2]
    block_width = partials.shape[3]
    fsdp_count = lax.axis_size("fsdp")
    per_slice = block_total // lax.axis_size("rep")
    slot_count = sketch.shape[2]
    reduced = lax.psum_scatter(
        partials[0].astype(jnp.float32).astype(jnp.bfloat16), "rep", scatter_dimension=0, tiled=True
    )
    my_owners = lax.dynamic_slice_in_dim(
        owner_table[:, 0], lax.axis_index("rep") * per_slice, per_slice
    )
    positions = jnp.arange(per_slice, dtype=jnp.int32)
    same_owner = (my_owners[:, None] == my_owners[None, :]) & (
        positions[:, None] < positions[None, :]
    )
    rank_in = jnp.sum(same_owner.astype(jnp.int32), axis=0)
    target = rank_in * fsdp_count + my_owners
    selector = (
        target[None, :] == jnp.arange(slot_count * fsdp_count, dtype=jnp.int32)[:, None]
    ).astype(jnp.bfloat16)
    flattened = reduced.reshape(per_slice, row_count * block_width)
    outgoing = jnp.dot(selector, flattened, preferred_element_type=jnp.float32).astype(jnp.bfloat16)
    outgoing = outgoing.reshape(slot_count, fsdp_count, row_count, block_width)
    sum_squares = lax.psum(squared_sum(reduced), ("fsdp", "rep"))
    clip_limit = 0.5 * math.sqrt(block_total * block_width * block_width)
    clip_factor = jnp.minimum(1.0, clip_limit / jnp.sqrt(sum_squares + 1e-06))
    filled = jnp.sum((my_owners == lax.axis_index("fsdp")).astype(jnp.int32))
    held_sketches = sketch[0, 0]
    fresh_list = []
    incoming = lax.all_to_all(outgoing, "fsdp", split_axis=1, concat_axis=1, tiled=True)
    update_list = []
    for slot_index in range(slot_count):
        update_block, new_block = process_slot(
            slot_index, incoming[slot_index], clip_factor, held_sketches, filled
        )
        update_list.append(update_block)
        fresh_list.append(new_block)
    stacked = jnp.stack(update_list).reshape(slot_count, fsdp_count, row_count, block_width)
    returned = lax.all_to_all(stacked, "fsdp", split_axis=1, concat_axis=1, tiled=True)
    returned = returned.reshape(slot_count * fsdp_count, row_count * block_width)
    my_updates = lax.dot_general(
        selector, returned, FIRST_AXES, preferred_element_type=jnp.float32
    ).astype(jnp.bfloat16)
    my_updates = my_updates.reshape(per_slice, row_count, block_width)
    return (my_updates, jnp.stack(fresh_list)[None, None])


def solution(mesh):
    placed = (P("rep", None, "fsdp", None), P("fsdp", "rep", None, None, None), P())
    return jax.shard_map(
        local,
        mesh=mesh,
        in_specs=placed,
        out_specs=(P("rep", "fsdp", None), P("fsdp", "rep", None, None, None)),
        check_vma=False,
    )
```

profile of v0, /device:TPU:0, one launch (start us, length us, event | category | flops | bytes accessed | tf_op | source)
XLA Modules:
  0.0 441.0 jit_solution(7717073570326933660)
XLA Ops:
  7.9 0.8 fusion.55
  8.8 118.5 %reduce-scatter.2.cloned.1.call-done = bf16[14,128,1024]{2,1,0:T(8,128)(2,1)} async-done(((bf16[56,128,1024]{2,1,0:T(8,128)(2,1)}), bf16[14,128,1024]{2,1,0:T(8,128)(2,1)}) %reduce-scatter.2.cloned.1.call-update) | async-done | bytes 3670032 | tf_op jit(solution)/shard_map/reduce_scatter | solution.py:89
  127.3 2.5 pad.4
  129.8 2.3 copy.28
  132.1 1.2 convolution_convert_fusion.1
  133.3 4.3 copy.20
  137.6 5.5 %all-to-all-start = ((bf16[2,8,128,1024]{3,2,0,1:T(8,128)(2,1)}), bf16[2,8,128,1024]{3,2,0,1:T(8,128)(2,1)}, u32[]{:S(2)}, u32[]{:S(2)}) async-start(bf16[2,8,128,1024]{3,2,0,1:T(8,128)(2,1)} %copy.20), calls=%async_computation.1 | async-start | bytes 8388608 | tf_op jit(solution)/shard_map/all_to_all | solution.py:113
  143.1 4.5 %multiply_reduce_fusion = f32[]{:T(128)} fusion(bf16[14,128,1024]{2,1,0:T(8,128)(2,1)} %reduce-scatter.2.cloned.1.call-done), kind=kLoop, calls=%fused_computation.2 | loop fusion | flops 5505023 | bytes 3670020 | tf_op jit(solution)/shard_map/reduce_sum | solution.py:67
  147.7 108.8 %psum.7 = f32[]{:T(128)} all-reduce(f32[]{:T(128)} %multiply_reduce_fusion), channel_id=1, replica_groups=mesh['fsdp'=8,'rep'=4] {'fsdp','rep'}, use_global_device_ids=true, to_apply=%region_3.0 | all-reduce | flops 1 | bytes 8 | tf_op jit(solution)/shard_map/psum | solution.py:107
  257.2 4.9 %multiply_convert_fusion.1 = (bf16[1,8,128,1024]{3,2,0,1:T(8,128)(2,1)}, bf16[1,8,128,1024]{3,2,0,1:T(8,128)(2,1)S(1)}) fusion(bf16[2,8,128,1024]{3,2,0,1:T(8,128)(2,1)} %all-to-all-done, f32[]{:T(128)S(6)} %min_shard_map.3), kind=kLoop, calls=%fused_computation.8 | loop fusion | flops 6291456 | bytes 8388612 | tf_op jit(solution)/shard_map/convert_element_type | solution.py:72
  262.1 1.3 copy-done.5
  263.5 3.3 fusion.11
  266.7 2.1 fusion.1
  268.8 1.6 select_reduce_fusion.1
  276.4 1.8 fusion.92
  278.6 1.0 convolution_convert_fusion.6
  279.6 0.8 copy-done.8
  280.7 1.0 select_reduce_fusion
  282.4 1.0 select_subtract_fusion.4
  283.4 1.0 fusion.46
  287.8 1.1 fusion.99
  288.9 5.5 %fusion.10 = f32[1024,256]{0,1:T(8,128)} fusion(bf16[1024,1024]{1,0:T(8,128)(2,1)} %bitcast.197, bf16[1,1,2,1024,256]{4,3,2,1,0:T(8,128)(2,1)S(1)} %copy-done), kind=kOutput, calls=%fused_computation.77 | convolution fusion | flops 1074003968 | bytes 5767168 | tf_op jit(solution)/shard_map/dot_general | solution.py:36
  294.5 2.1 fusion.3
  296.5 2.4 select_reduce_fusion.3
  299.6 1.3 select_subtract_fusion.19
  300.9 1.3 fusion.44
  304.8 0.8 select_subtract_fusion.16
  307.2 1.8 fusion.78
  309.4 0.8 convolution_convert_fusion.8
  310.5 1.0 select_reduce_fusion.2
  312.2 0.9 select_subtract_fusion.14
  313.1 1.0 fusion.49
  318.7 0.7 copy-done.13
  320.1 0.7 add_convert_fusion
  322.4 0.7 add_convert_fusion.1
  323.2 2.3 pad_maximum_fusion
  325.5 4.7 %all-to-all-start.1 = ((bf16[2,8,128,1024]{3,2,0,1:T(8,128)(2,1)}), bf16[2,8,128,1024]{3,2,0,1:T(8,128)(2,1)}, u32[]{:S(2)}, u32[]{:S(2)}) async-start(bf16[2,8,128,1024]{3,2,0,1:T(8,128)(2,1)} %pad_maximum_fusion), calls=%async_computation.2 | async-start | bytes 8388608 | tf_op jit(solution)/shard_map/all_to_all | solution.py:122
  331.6 1.3 fusion.101
  332.9 1.0 fusion.7
  333.9 1.4 fusion.100
  335.4 1.0 fusion.5
  336.4 1.1 maximum_bitcast_fusion
  337.4 85.5 %all-to-all-done.1 = bf16[2,8,128,1024]{3,2,0,1:T(8,128)(2,1)} async-done(((bf16[2,8,128,1024]{3,2,0,1:T(8,128)(2,1)}), bf16[2,8,128,1024]{3,2,0,1:T(8,128)(2,1)}, u32[]{:S(2)}, u32[]{:S(2)}) %all-to-all-start.1) | async-done | bytes 4194336 | tf_op jit(solution)/shard_map/all_to_all | solution.py:122
  422.9 2.6 copy.32
  425.5 2.3 copy.29
  427.9 1.5 convolution_convert_fusion
  429.4 2.3 copy.30
  431.7 2.2 slice.20
  (94 shorter events, 21.4 us)
Async XLA Ops:
  7.2 120.1 %reduce-scatter.2.cloned.1.call-start = ((), (), s32[]{:S(2)}) async-start(), calls=%async_computation.3 | async-start | bytes 18350080 | tf_op jit(solution)/shard_map/reduce_scatter | solution.py:89
  7.2 0.7 copy-start.18
  137.6 119.5 %all-to-all-start = ((bf16[2,8,128,1024]{3,2,0,1:T(8,128)(2,1)}), bf16[2,8,128,1024]{3,2,0,1:T(8,128)(2,1)}, u32[]{:S(2)}, u32[]{:S(2)}) async-start(bf16[2,8,128,1024]{3,2,0,1:T(8,128)(2,1)} %copy.20), calls=%async_computation.1 | async-start | bytes 8388608 | tf_op jit(solution)/shard_map/all_to_all | solution.py:113
  257.1 6.3 %copy-start = (bf16[1,1,2,1024,256]{4,3,2,1,0:T(8,128)(2,1)S(1)}, bf16[1,1,2,1024,256]{4,3,2,1,0:T(8,128)(2,1)}, u32[]{:S(2)}) copy-start(bf16[1,1,2,1024,256]{4,3,2,1,0:T(8,128)(2,1)} %param.4) | copy-start | bytes 3145732
  262.1 1.3 copy-start.5
  274.4 4.1 copy-start.6
  279.6 0.8 copy-start.8
  281.7 5.7 %copy-start.16 = (f32[256,256]{1,0:T(8,128)}, f32[256,256]{1,0:T(8,128)S(1)}, u32[]{:S(2)}) copy-start(f32[256,256]{1,0:T(8,128)S(1)} %get-tuple-element.9) | copy-start | bytes 786436
  304.8 4.5 %copy-start.3 = (bf16[1,8,128,1024]{3,2,0,1:T(8,128)(2,1)S(1)}, bf16[1,8,128,1024]{3,2,0,1:T(8,128)(2,1)}, u32[]{:S(2)}) copy-start(bf16[1,8,128,1024]{3,2,0,1:T(8,128)(2,1)} %get-tuple-element.4) | copy-start | bytes 6291460
  309.0 1.5 copy-start.1
  310.2 1.4 copy-start.10
  311.5 5.5 %copy-start.17 = (f32[256,256]{1,0:T(8,128)}, f32[256,256]{1,0:T(8,128)S(1)}, u32[]{:S(2)}) copy-start(f32[256,256]{1,0:T(8,128)S(1)} %get-tuple-element.13) | copy-start | bytes 786436
  313.1 4.8 %copy-start.12 = (f32[256,256]{1,0:T(8,128)S(1)}, f32[256,256]{1,0:T(8,128)}, u32[]{:S(2)}) copy-start(f32[256,256]{1,0:T(8,128)} %fusion.99) | copy-start | bytes 786436
  314.7 4.6 %copy-start.9 = (bf16[1024,256]{1,0:T(8,128)(2,1)S(1)}, bf16[1024,256]{1,0:T(8,128)(2,1)}, u32[]{:S(2)}) copy-start(bf16[1024,256]{1,0:T(8,128)(2,1)} %copy-done.8) | copy-start | bytes 1572868
  315.1 4.9 %copy-start.7 = (bf16[1,8,128,1024]{3,2,0,1:T(8,128)(2,1)S(1)}, bf16[1,8,128,1024]{3,2,0,1:T(8,128)(2,1)}, u32[]{:S(2)}) copy-start(bf16[1,8,128,1024]{3,2,0,1:T(8,128)(2,1)} %copy-done.5) | copy-start | bytes 6291460
  318.7 0.7 copy-start.13
  319.4 2.2 copy-start.11
  320.0 2.4 copy-start.2
  320.0 2.4 copy-start.4
  321.6 1.6 copy-start.15
  325.5 6.1 %copy-start.14 = (f32[256,256]{1,0:T(8,128)S(1)}, f32[256,256]{1,0:T(8,128)}, u32[]{:S(2)}) copy-start(f32[256,256]{1,0:T(8,128)} %copy-done.13) | copy-start | bytes 786436
  325.5 97.4 %all-to-all-start.1 = ((bf16[2,8,128,1024]{3,2,0,1:T(8,128)(2,1)}), bf16[2,8,128,1024]{3,2,0,1:T(8,128)(2,1)}, u32[]{:S(2)}, u32[]{:S(2)}) async-start(bf16[2,8,128,1024]{3,2,0,1:T(8,128)(2,1)} %pad_maximum_fusion), calls=%async_computation.2 | async-start | bytes 8388608 | tf_op jit(solution)/shard_map/all_to_all | solution.py:122
Sparse Core Ops, SparseCore 0:
  10.6 116.6 reduce-scatter.1
where the time goes:
time: 448 us; the launch traced here: 441 us
  waiting for transfers between devices  205 us (46%)
  blocking collectives  109 us (24%)
  matrix products  62.1 us (14%)
  local copies, waits for them, and re-layouts  21.7 us (5%)
  between operations  19.8 us (4%)
  other arithmetic  13.8 us (3%)
  starting transfers between devices  10.2 us (2%)
    reduce_scatter x1, waiting for transfers between devices, local(): lax.psum_scatter(partials[0].astype(jnp.float32).astype(jnp.bfloat16), 'r...  118 us
    psum x1, blocking collectives, local(): sum_squares = lax.psum(squared_sum(reduced), ('fsdp', 'rep'))  109 us
    all_to_all x1, waiting for transfers between devices, local(): lax.all_to_all(stacked, 'fsdp', split_axis=1, concat_axis=1, tiled=True)  85.5 us
    unnamed x42, local copies, waits for them, and re-layouts  12.5 us
    dot_general x20, matrix products, inverse_root(): jnp.dot(inverse, current, precision=lax.Precision.HIGHEST)  9.95 us
    dot_general x16, matrix products, inverse_root(): current = jnp.dot(current, middle, precision=lax.Precision.HIGHEST)  8.99 us
  transfers between devices with their start and end apart: 3, of which 2 were waited for; matrix products, arithmetic and copies ran while one was open for 3% of the time, Pallas kernels for 0%

commit v1 on v0

--- a/solution.py
+++ b/solution.py
@@ -104,7 +104,9 @@
     flattened = reduced.reshape(per_slice, row_count * block_width)
     outgoing = jnp.dot(selector, flattened, preferred_element_type=jnp.float32).astype(jnp.bfloat16)
     outgoing = outgoing.reshape(slot_count, fsdp_count, row_count, block_width)
-    sum_squares = lax.psum(squared_sum(reduced), ("fsdp", "rep"))
+    sum_squares = squared_sum(reduced)
+    for name in ("rep", "fsdp"):
+        sum_squares = lax.psum(sum_squares, name)
     clip_limit = 0.5 * math.sqrt(block_total * block_width * block_width)
     clip_factor = jnp.minimum(1.0, clip_limit / jnp.sqrt(sum_squares + 1e-06))
     filled = jnp.sum((my_owners == lax.axis_index("fsdp")).astype(jnp.int32))

time: 448 us -> 434 us (0.969)
  blocking collectives: 109 us -> 80.9 us
  starting transfers between devices: 10.2 us -> 18.8 us
  waiting for transfers between devices: 205 us -> 210 us
    psum x1 -> x2, blocking collectives: 109 us -> 80.9 us  [local(): sum_squares = lax.psum(sum_squares, name)]
    all_to_all x1, starting transfers between devices: 4.67 us -> 13.3 us  [local(): lax.all_to_all(stacked, 'fsdp', split_axis=1, concat_axis=1, tiled=True)]
    all_to_all x1, waiting for transfers between devices: 0.01 us -> 7.04 us  [local(): lax.all_to_all(outgoing, 'fsdp', split_axis=1, concat_axis=1, tiled=True)]
  transfers between devices with their start and end apart: 3 -> 3, of which waited for: 2 -> 3; matrix products, arithmetic and copies ran while one was open for 3% -> 3% of each run, Pallas kernels for 0% -> 0%
where the time goes in v1:
time: 434 us; the launch traced here: 427 us
  waiting for transfers between devices  210 us (48%)
  blocking collectives  80.9 us (19%)
  matrix products  62.3 us (14%)
  local copies, waits for them, and re-layouts  21.5 us (5%)
  between operations  19.9 us (5%)
  starting transfers between devices  18.8 us (4%)
  other arithmetic  13.6 us (3%)
    reduce_scatter x1, waiting for transfers between devices, local(): lax.psum_scatter(partials[0].astype(jnp.float32).astype(jnp.bfloat16), 'r...  119 us
    all_to_all x1, waiting for transfers between devices, local(): lax.all_to_all(stacked, 'fsdp', split_axis=1, concat_axis=1, tiled=True)  83.5 us
    psum x2, blocking collectives, local(): sum_squares = lax.psum(sum_squares, name)  80.9 us
    all_to_all x1, starting transfers between devices, local(): lax.all_to_all(stacked, 'fsdp', split_axis=1, concat_axis=1, tiled=True)  13.3 us
    unnamed x42, local copies, waits for them, and re-layouts  12.4 us
    dot_general x20, matrix products, inverse_root(): jnp.dot(inverse, current, precision=lax.Precision.HIGHEST)  10 us
    dot_general x16, matrix products, inverse_root(): current = jnp.dot(current, middle, precision=lax.Precision.HIGHEST)  9.07 us
    dot_general x2, matrix products, precondition(): jnp.dot(gradient, projected, preferred_element_type=jnp.float32)  8.78 us
  transfers between devices with their start and end apart: 3, of which 3 were waited for; matrix products, arithmetic and copies ran while one was open for 3% of the time, Pallas kernels for 0%

profile of v1, /device:TPU:0, one launch (start us, length us, event | category | flops | bytes accessed | tf_op | source)
XLA Modules:
  0.0 426.8 jit_solution(8475079314243421791)
XLA Ops:
  8.7 118.5 %reduce-scatter.2.cloned.1.call-done = bf16[14,128,1024]{2,1,0:T(8,128)(2,1)} async-done(((bf16[56,128,1024]{2,1,0:T(8,128)(2,1)}), bf16[14,128,1024]{2,1,0:T(8,128)(2,1)}) %reduce-scatter.2.cloned.1.call-update) | async-done | bytes 3670032 | tf_op jit(solution)/shard_map/reduce_scatter | solution.py:89
  127.3 2.5 pad.4
  129.8 2.3 copy.28
  132.1 1.2 convolution_convert_fusion.1
  133.3 4.3 %copy.20 = bf16[2,8,128,1024]{3,2,0,1:T(8,128)(2,1)} copy(bf16[2,8,128,1024]{3,1,2,0:T(8,128)(2,1)S(1)} %bitcast.193) | data formatting | bytes 8388608 | tf_op jit(solution)/shard_map/reshape | solution.py:106
  137.6 5.5 %all-to-all-start = ((bf16[2,8,128,1024]{3,2,0,1:T(8,128)(2,1)}), bf16[2,8,128,1024]{3,2,0,1:T(8,128)(2,1)}, u32[]{:S(2)}, u32[]{:S(2)}) async-start(bf16[2,8,128,1024]{3,2,0,1:T(8,128)(2,1)} %copy.20), calls=%async_computation.1 | async-start | bytes 8388608 | tf_op jit(solution)/shard_map/all_to_all | solution.py:115
  143.1 4.5 %multiply_reduce_fusion = f32[]{:T(128)} fusion(bf16[14,128,1024]{2,1,0:T(8,128)(2,1)} %reduce-scatter.2.cloned.1.call-done), kind=kLoop, calls=%fused_computation.2 | loop fusion | flops 5505023 | bytes 3670020 | tf_op jit(solution)/shard_map/reduce_sum | solution.py:67
  147.7 6.7 %psum.14 = f32[]{:T(128)} all-reduce(f32[]{:T(128)} %multiply_reduce_fusion), channel_id=1, replica_groups=mesh['fsdp'=8,'rep'=4] {'rep'}, use_global_device_ids=true, to_apply=%region_3.0 | all-reduce | flops 1 | bytes 8 | tf_op jit(solution)/shard_map/psum | solution.py:109
  154.3 74.3 %psum.15 = f32[]{:T(128)} all-reduce(f32[]{:T(128)} %psum.14), channel_id=1, replica_groups=mesh['fsdp'=8,'rep'=4] {'fsdp'}, use_global_device_ids=true, to_apply=%region_4.0 | all-reduce | flops 1 | bytes 8 | tf_op jit(solution)/shard_map/psum | solution.py:109
  229.3 7.0 %all-to-all-done = bf16[2,8,128,1024]{3,2,0,1:T(8,128)(2,1)} async-done(((bf16[2,8,128,1024]{3,2,0,1:T(8,128)(2,1)}), bf16[2,8,128,1024]{3,2,0,1:T(8,128)(2,1)}, u32[]{:S(2)}, u32[]{:S(2)}) %all-to-all-start) | async-done | bytes 4194336 | tf_op jit(solution)/shard_map/all_to_all | solution.py:115
  236.3 4.9 %multiply_convert_fusion.1 = (bf16[1,8,128,1024]{3,2,0,1:T(8,128)(2,1)}, bf16[1,8,128,1024]{3,2,0,1:T(8,128)(2,1)S(1)}) fusion(bf16[2,8,128,1024]{3,2,0,1:T(8,128)(2,1)} %all-to-all-done, f32[]{:T(128)S(6)} %min_shard_map.3), kind=kLoop, calls=%fused_computation.8 | loop fusion | flops 6291456 | bytes 8388612 | tf_op jit(solution)/shard_map/convert_element_type | solution.py:72
  241.2 1.3 copy-done.5
  242.5 3.3 fusion.11
  245.8 2.1 fusion.1
  247.9 1.6 select_reduce_fusion.1
  255.5 1.8 fusion.92
  257.6 1.0 convolution_convert_fusion.6
  258.7 0.8 copy-done.8
  259.8 1.0 select_reduce_fusion
  261.5 1.0 select_subtract_fusion.4
  262.5 1.0 fusion.46
  266.9 1.1 fusion.99
  268.0 5.5 %fusion.10 = f32[1024,256]{0,1:T(8,128)} fusion(bf16[1024,1024]{1,0:T(8,128)(2,1)} %bitcast.197, bf16[1,1,2,1024,256]{4,3,2,1,0:T(8,128)(2,1)S(1)} %copy-done), kind=kOutput, calls=%fused_computation.77 | convolution fusion | flops 1074003968 | bytes 5767168 | tf_op jit(solution)/shard_map/dot_general | solution.py:36
  273.5 2.1 fusion.3
  275.6 2.4 select_reduce_fusion.3
  278.7 1.3 select_subtract_fusion.19
  280.0 1.3 fusion.44
  284.0 0.8 select_subtract_fusion.16
  286.3 1.8 fusion.78
  288.5 0.8 convolution_convert_fusion.8
  289.6 1.0 select_reduce_fusion.2
  291.4 1.0 select_subtract_fusion.14
  292.4 1.1 fusion.49
  299.4 0.7 add_convert_fusion
  301.8 0.7 add_convert_fusion.1
  302.6 2.3 pad_maximum_fusion
  304.9 13.3 %all-to-all-start.1 = ((bf16[2,8,128,1024]{3,2,0,1:T(8,128)(2,1)}), bf16[2,8,128,1024]{3,2,0,1:T(8,128)(2,1)}, u32[]{:S(2)}, u32[]{:S(2)}) async-start(bf16[2,8,128,1024]{3,2,0,1:T(8,128)(2,1)} %pad_maximum_fusion), calls=%async_computation.2 | async-start | bytes 8388608 | tf_op jit(solution)/shard_map/all_to_all | solution.py:124
  319.4 1.3 fusion.101
  320.7 1.0 fusion.7
  321.7 1.4 fusion.100
  323.2 1.0 fusion.5
  324.2 1.1 maximum_bitcast_fusion
  325.2 83.5 %all-to-all-done.1 = bf16[2,8,128,1024]{3,2,0,1:T(8,128)(2,1)} async-done(((bf16[2,8,128,1024]{3,2,0,1:T(8,128)(2,1)}), bf16[2,8,128,1024]{3,2,0,1:T(8,128)(2,1)}, u32[]{:S(2)}, u32[]{:S(2)}) %all-to-all-start.1) | async-done | bytes 4194336 | tf_op jit(solution)/shard_map/all_to_all | solution.py:124
  408.7 2.6 copy.32
  411.4 2.3 copy.29
  413.7 1.5 convolution_convert_fusion
  415.2 2.3 copy.30
  417.6 2.2 slice.20
  (95 shorter events, 22.7 us)
Async XLA Ops:
  7.2 120.1 %reduce-scatter.2.cloned.1.call-start = ((), (), s32[]{:S(2)}) async-start(), calls=%async_computation.3 | async-start | bytes 18350080 | tf_op jit(solution)/shard_map/reduce_scatter | solution.py:89
  7.2 0.7 copy-start.18
  137.6 98.7 %all-to-all-start = ((bf16[2,8,128,1024]{3,2,0,1:T(8,128)(2,1)}), bf16[2,8,128,1024]{3,2,0,1:T(8,128)(2,1)}, u32[]{:S(2)}, u32[]{:S(2)}) async-start(bf16[2,8,128,1024]{3,2,0,1:T(8,128)(2,1)} %copy.20), calls=%async_computation.1 | async-start | bytes 8388608 | tf_op jit(solution)/shard_map/all_to_all | solution.py:115
  229.3 13.2 %copy-start = (bf16[1,1,2,1024,256]{4,3,2,1,0:T(8,128)(2,1)S(1)}, bf16[1,1,2,1024,256]{4,3,2,1,0:T(8,128)(2,1)}, u32[]{:S(2)}) copy-start(bf16[1,1,2,1024,256]{4,3,2,1,0:T(8,128)(2,1)} %param.4) | copy-start | bytes 3145732
  241.2 1.3 copy-start.5
  253.5 4.1 copy-start.6
  258.7 0.8 copy-start.8
  260.8 5.7 %copy-start.16 = (f32[256,256]{1,0:T(8,128)}, f32[256,256]{1,0:T(8,128)S(1)}, u32[]{:S(2)}) copy-start(f32[256,256]{1,0:T(8,128)S(1)} %get-tuple-element.9) | copy-start | bytes 786436
  284.0 4.5 %copy-start.3 = (bf16[1,8,128,1024]{3,2,0,1:T(8,128)(2,1)S(1)}, bf16[1,8,128,1024]{3,2,0,1:T(8,128)(2,1)}, u32[]{:S(2)}) copy-start(bf16[1,8,128,1024]{3,2,0,1:T(8,128)(2,1)} %get-tuple-element.4) | copy-start | bytes 6291460
  288.1 1.5 copy-start.1
  289.3 1.4 copy-start.10
  290.7 5.8 %copy-start.17 = (f32[256,256]{1,0:T(8,128)}, f32[256,256]{1,0:T(8,128)S(1)}, u32[]{:S(2)}) copy-start(f32[256,256]{1,0:T(8,128)S(1)} %get-tuple-element.13) | copy-start | bytes 786436
  292.4 4.9 %copy-start.12 = (f32[256,256]{1,0:T(8,128)S(1)}, f32[256,256]{1,0:T(8,128)}, u32[]{:S(2)}) copy-start(f32[256,256]{1,0:T(8,128)} %fusion.99) | copy-start | bytes 786436
  294.1 4.6 %copy-start.9 = (bf16[1024,256]{1,0:T(8,128)(2,1)S(1)}, bf16[1024,256]{1,0:T(8,128)(2,1)}, u32[]{:S(2)}) copy-start(bf16[1024,256]{1,0:T(8,128)(2,1)} %copy-done.8) | copy-start | bytes 1572868
  294.5 4.9 %copy-start.7 = (bf16[1,8,128,1024]{3,2,0,1:T(8,128)(2,1)S(1)}, bf16[1,8,128,1024]{3,2,0,1:T(8,128)(2,1)}, u32[]{:S(2)}) copy-start(bf16[1,8,128,1024]{3,2,0,1:T(8,128)(2,1)} %copy-done.5) | copy-start | bytes 6291460
  298.0 0.7 copy-start.13
  298.7 2.2 copy-start.11
  299.4 2.4 copy-start.2
  299.4 2.4 copy-start.4
  301.0 1.6 copy-start.15
  304.9 14.5 %copy-start.14 = (f32[256,256]{1,0:T(8,128)S(1)}, f32[256,256]{1,0:T(8,128)}, u32[]{:S(2)}) copy-start(f32[256,256]{1,0:T(8,128)} %copy-done.13) | copy-start | bytes 786436
  304.9 103.8 %all-to-all-start.1 = ((bf16[2,8,128,1024]{3,2,0,1:T(8,128)(2,1)}), bf16[2,8,128,1024]{3,2,0,1:T(8,128)(2,1)}, u32[]{:S(2)}, u32[]{:S(2)}) async-start(bf16[2,8,128,1024]{3,2,0,1:T(8,128)(2,1)} %pad_maximum_fusion), calls=%async_computation.2 | async-start | bytes 8388608 | tf_op jit(solution)/shard_map/all_to_all | solution.py:124
Sparse Core Ops, SparseCore 0:
  10.6 116.6 reduce-scatter.1
